TPU v7x, 32 devices: a whole 2x2x4 slice. The times are simulated.
32 devices in a mesh: dp: 4 (over x, core), fsdp: 8 (over z, y).
Axes of the slice: x: 2, y: 2, z: 4, core: 2. Of those that a mesh axis runs over, the one named last changes fastest.
Arguments:
- text_rows: bfloat16 [64, 512, 768], P(('dp', 'fsdp')), may hold values from -6 to 6
- visual_matrix: bfloat16 [768, 768], P('fsdp'), may hold values from -0.21875 to 0.21875
- batch_gain: bfloat16 [768], P('fsdp'), may hold values from 0.5 to 1.5
- batch_shift: bfloat16 [768], P('fsdp'), may hold values from -2.5 to 2.5
- attend_weight: bfloat16 [768, 2304], P('fsdp'), may hold values from -0.21875 to 0.21875
- merge_weight: bfloat16 [768, 768], P('fsdp'), may hold values from -1.75 to 1.75
- first_gain: bfloat16 [768], P('fsdp'), may hold values from 0.5 to 1.5
- first_shift: bfloat16 [768], P('fsdp'), may hold values from -2.5 to 2.5
- up_matrix: bfloat16 [768, 3072], P('fsdp'), may hold values from -0.21875 to 0.21875
- down_matrix: bfloat16 [3072, 768], P('fsdp'), may hold values from -0.109375 to 0.109375
- second_gain: bfloat16 [768], P('fsdp'), may hold values from 0.5 to 1.5
- second_shift: bfloat16 [768], P('fsdp'), may hold values from -2.5 to 2.5
- segment_counts: int32 [64], P(('dp', 'fsdp')), may hold values from 5 to 128, as said below
- segment_ids: int32 [64, 512], P(('dp', 'fsdp')), may hold values from -1 to 127, as said below
- padding_mask: int32 [64, 512], P(('dp', 'fsdp')), may hold values from 0 to 1, as said below
- cotangent: bfloat16 [64, 512, 768], P(('dp', 'fsdp')), may hold values from -6 to 6
Outputs:
- layer_output: float32 [64, 512, 768], P(('dp', 'fsdp'))
- text_gradient: float32 [64, 512, 768], P(('dp', 'fsdp'))
- visual_gradient: float32 [768, 768], P('fsdp')
- batch_gain_gradient: float32 [768], P('fsdp')
- batch_shift_gradient: float32 [768], P('fsdp')
- attend_gradient: float32 [768, 2304], P('fsdp')
- merge_gradient: float32 [768, 768], P('fsdp')
- first_gain_gradient: float32 [768], P('fsdp')
- first_shift_gradient: float32 [768], P('fsdp')
- up_gradient: float32 [768, 3072], P('fsdp')
- down_gradient: float32 [3072, 768], P('fsdp')
- second_gain_gradient: float32 [768], P('fsdp')
- second_shift_gradient: float32 [768], P('fsdp')
Inputs may be any that keep to these rules, and one draw needn't show every extreme that they name: On every device of dp+fsdp one of its documents has exactly 128 segments; segment_counts[d] is one more than the largest segment_ids in document d. `segment_ids`: A document's real rows come first and form segment_counts consecutive runs of one or more rows, numbered 0, 1, ... in order; padding rows hold -1. `padding_mask`: 1 exactly on the rows whose segment id is not -1, which are the first 256 or more rows of a document.
All inputs are finite; a program needn't handle non-finite values.
Results may differ from a plain program's by a relative error of at most 0.023.
The roundings to bfloat16 on the way count: a program that leaves them out, or rounds other values in their place, can miss the bound.
Values may be sent and summed in bfloat16 or wider, within the bound.
No kernel may reach another device: no remote copies, remote signals or barrier semaphores. Data moves between devices by JAX's collectives and lax.ppermute only.
A program may use at most 192 MiB of HBM per device.

v0:
```python
import jax
import jax.numpy as jnp
from jax import lax
from jax.sharding import PartitionSpec as P

HEADS = 12
SEGMAX = 128
eps_norm = 1e-05
eps_batch = 1e-05
masked_score = -1e30
highest_precision = lax.Precision.HIGHEST


def layer_norm(values, gain, shift):
    center = values - jnp.mean(values, axis=-1, keepdims=True)
    variance = jnp.mean(center * center, axis=-1, keepdims=True)
    return center * lax.rsqrt(variance + eps_norm) * gain + shift


def exact_gelu(values):
    return jax.nn.gelu(values, approximate=False)


def split_heads(packed):
    length = packed.shape[0]
    features = packed.shape[1] // 3
    head_size = features // HEADS
    queries = packed[:, :features].reshape(length, HEADS, head_size)
    keys_part = packed[:, features : 2 * features].reshape(length, HEADS, head_size)
    values_part = packed[:, 2 * features :].reshape(length, HEADS, head_size)
    return (queries, keys_part, values_part, head_size ** (-0.5))


def masked_scores(queries, keys_part, key_mask, scaling):
    scores = (
        jnp.einsum("qhe,khe->hqk", queries, keys_part, preferred_element_type=jnp.float32) * scaling
    )
    return jnp.where(key_mask[None, None, :] > 0, scores, masked_score)


def attend_doc(operands):
    packed, key_mask = operands
    queries, keys_part, values_part, scaling = split_heads(packed)
    scores = masked_scores(queries, keys_part, key_mask, scaling)
    top_score = jnp.max(scores, axis=-1, keepdims=True)
    unnormed = jnp.exp(scores - top_score)
    totals = jnp.sum(unnormed, axis=-1, keepdims=True)
    attention = unnormed / totals
    mixed = jnp.einsum(
        "hqk,khe->qhe",
        attention.astype(jnp.bfloat16),
        values_part,
        preferred_element_type=jnp.float32,
    )
    log_total = (top_score + jnp.log(totals))[..., 0]
    return (mixed.reshape(packed.shape[0], packed.shape[1] // 3).astype(jnp.bfloat16), log_total)


def attend_back(operands):
    packed, key_mask, log_total, delta_attended = operands
    queries, keys_part, values_part, scaling = split_heads(packed)
    length = packed.shape[0]
    features = packed.shape[1] // 3
    scores = masked_scores(queries, keys_part, key_mask, scaling)
    attention = jnp.exp(scores - log_total[..., None])
    delta_heads = delta_attended.reshape(length, HEADS, features // HEADS)
    delta_attention = jnp.einsum(
        "qhe,khe->hqk", delta_heads, values_part, preferred_element_type=jnp.float32
    )
    delta_scores = attention * (
        delta_attention - jnp.sum(attention * delta_attention, axis=-1, keepdims=True)
    )
    delta_low = delta_scores.astype(jnp.bfloat16)
    delta_queries = (
        jnp.einsum("hqk,khe->qhe", delta_low, keys_part, preferred_element_type=jnp.float32)
        * scaling
    )
    delta_keys = (
        jnp.einsum("hqk,qhe->khe", delta_low, queries, preferred_element_type=jnp.float32) * scaling
    )
    delta_values = jnp.einsum(
        "hqk,qhe->khe",
        attention.astype(jnp.bfloat16),
        delta_heads,
        preferred_element_type=jnp.float32,
    )
    merged = jnp.concatenate(
        [
            delta_queries.reshape(length, features),
            delta_keys.reshape(length, features),
            delta_values.reshape(length, features),
        ],
        axis=1,
    )
    return merged.astype(jnp.bfloat16)


def shards(
    text_rows,
    visual_matrix,
    batch_gain,
    batch_shift,
    attend_weight,
    merge_weight,
    first_gain,
    first_shift,
    up_matrix,
    down_matrix,
    second_gain,
    second_shift,
    segment_counts,
    segment_ids,
    padding_mask,
    cotangent,
):
    gathered = (
        lax.all_gather(visual_matrix, "fsdp", axis=0, tiled=True),
        lax.all_gather(batch_gain, "fsdp", axis=0, tiled=True),
        lax.all_gather(batch_shift, "fsdp", axis=0, tiled=True),
        lax.all_gather(attend_weight, "fsdp", axis=0, tiled=True),
        lax.all_gather(merge_weight, "fsdp", axis=0, tiled=True),
        lax.all_gather(first_gain, "fsdp", axis=0, tiled=True),
        lax.all_gather(first_shift, "fsdp", axis=0, tiled=True),
        lax.all_gather(up_matrix, "fsdp", axis=0, tiled=True),
        lax.all_gather(down_matrix, "fsdp", axis=0, tiled=True),
        lax.all_gather(second_gain, "fsdp", axis=0, tiled=True),
        lax.all_gather(second_shift, "fsdp", axis=0, tiled=True),
    )
    (
        gathered_visual_weight,
        full_batch_gain,
        full_batch_shift,
        full_attend,
        full_merge,
        full_first_gain,
        full_first_shift,
        gathered_up_weight,
        gathered_down_weight,
        full_second_gain,
        full_second_shift,
    ) = gathered
    features = text_rows.shape[2]
    slot_index = jnp.arange(SEGMAX)
    matches = segment_ids[:, :, None] == slot_index[None, None, :]
    onehot = matches.astype(jnp.bfloat16)
    onehot_wide = matches.astype(jnp.float32)
    divisor = jnp.maximum(jnp.sum(onehot_wide, axis=1), 1.0)[..., None]
    pooled_segments = (
        jnp.einsum("drs,drc->dsc", onehot, text_rows, preferred_element_type=jnp.float32) / divisor
    ).astype(jnp.bfloat16)
    visual_rows = jnp.einsum(
        "bil,ly->biy", pooled_segments, gathered_visual_weight, preferred_element_type=jnp.float32
    )
    valid_slot = (slot_index[None, :] < segment_counts[:, None]).astype(jnp.float32)[..., None]
    local_count = jnp.sum(segment_counts).astype(jnp.float32)
    masked_visual = valid_slot * visual_rows
    segment_total, visual_sum = lax.psum(
        (local_count, jnp.sum(masked_visual, axis=(0, 1))), ("dp", "fsdp")
    )
    batch_center = visual_sum / segment_total
    center = visual_rows - batch_center
    variance = (
        lax.psum(jnp.sum(valid_slot * center * center, axis=(0, 1)), ("dp", "fsdp")) / segment_total
    )
    inverse_spread = lax.rsqrt(variance + eps_batch)
    normed = center * inverse_spread
    embedded = (
        normed * full_batch_gain.astype(jnp.float32) + full_batch_shift.astype(jnp.float32)
    ).astype(jnp.bfloat16)
    joined = text_rows.astype(jnp.float32) + jnp.einsum(
        "drs,dsc->drc", onehot, embedded, preferred_element_type=jnp.float32
    )
    joined_low = joined.astype(jnp.bfloat16)
    packed = jnp.einsum(
        "drc,ce->dre", joined_low, full_attend, preferred_element_type=jnp.float32
    ).astype(jnp.bfloat16)
    attended, log_total = lax.map(attend_doc, (packed, padding_mask))
    projected = jnp.einsum("drc,ce->dre", attended, full_merge, preferred_element_type=jnp.float32)
    pre_one = joined + projected
    hidden_state = layer_norm(
        pre_one, full_first_gain.astype(jnp.float32), full_first_shift.astype(jnp.float32)
    )
    hidden_reduced_precision = hidden_state.astype(jnp.bfloat16)
    inner_hidden = jnp.einsum(
        "sjq,qy->sjy",
        hidden_reduced_precision,
        gathered_up_weight,
        preferred_element_type=jnp.float32,
    )
    gelu_activated = exact_gelu(inner_hidden).astype(jnp.bfloat16)
    residual_branch = jnp.einsum(
        "zya,av->zyv", gelu_activated, gathered_down_weight, preferred_element_type=jnp.float32
    )
    pre_two = hidden_state + residual_branch
    layer_output = layer_norm(
        pre_two, full_second_gain.astype(jnp.float32), full_second_shift.astype(jnp.float32)
    )
    again = (
        lax.all_gather(visual_matrix, "fsdp", axis=0, tiled=True),
        lax.all_gather(batch_gain, "fsdp", axis=0, tiled=True),
        lax.all_gather(attend_weight, "fsdp", axis=0, tiled=True),
        lax.all_gather(merge_weight, "fsdp", axis=0, tiled=True),
        lax.all_gather(first_gain, "fsdp", axis=0, tiled=True),
        lax.all_gather(up_matrix, "fsdp", axis=0, tiled=True),
        lax.all_gather(down_matrix, "fsdp", axis=0, tiled=True),
        lax.all_gather(second_gain, "fsdp", axis=0, tiled=True),
    )
    (
        visual_pullback,
        back_batch_gain,
        back_attend,
        back_merge,
        back_first_gain,
        up_pullback,
        down_pullback,
        back_second_gain,
    ) = again
    second_back = jax.vjp(
        layer_norm,
        pre_two,
        back_second_gain.astype(jnp.float32),
        full_second_shift.astype(jnp.float32),
    )[1]
    delta_two, second_gain_local, second_shift_local = second_back(cotangent.astype(jnp.float32))
    branch_gradient = delta_two.astype(jnp.bfloat16)
    down_local = jnp.einsum(
        "omt,oms->ts", gelu_activated, branch_gradient, preferred_element_type=jnp.float32
    )
    delta_activated = jnp.einsum(
        "ivj,hj->ivh", branch_gradient, down_pullback, preferred_element_type=jnp.float32
    )
    gelu_back = jax.vjp(exact_gelu, inner_hidden)[1]
    inner_gradient = gelu_back(delta_activated)[0].astype(jnp.bfloat16)
    up_local = jnp.einsum(
        "oih,oiu->hu", hidden_reduced_precision, inner_gradient, preferred_element_type=jnp.float32
    )
    delta_hidden = delta_two + jnp.einsum(
        "wmx,ix->wmi", inner_gradient, up_pullback, preferred_element_type=jnp.float32
    )
    first_back = jax.vjp(
        layer_norm,
        pre_one,
        back_first_gain.astype(jnp.float32),
        full_first_shift.astype(jnp.float32),
    )[1]
    delta_one, first_gain_local, first_shift_local = first_back(delta_hidden)
    delta_projected = delta_one.astype(jnp.bfloat16)
    merge_local = jnp.einsum(
        "drc,dre->ce", attended, delta_projected, preferred_element_type=jnp.float32
    )
    delta_attended = jnp.einsum(
        "dre,ce->drc", delta_projected, back_merge, preferred_element_type=jnp.float32
    ).astype(jnp.bfloat16)
    delta_packed = lax.map(attend_back, (packed, padding_mask, log_total, delta_attended))
    attend_local = jnp.einsum(
        "drc,dre->ce", joined_low, delta_packed, preferred_element_type=jnp.float32
    )
    delta_joined = delta_one + jnp.einsum(
        "dre,ce->drc", delta_packed, back_attend, preferred_element_type=jnp.float32
    )
    delta_embedded = jnp.einsum(
        "drs,drc->dsc",
        onehot_wide,
        delta_joined,
        precision=highest_precision,
        preferred_element_type=jnp.float32,
    )
    shift_total, gain_total = lax.psum(
        (jnp.sum(delta_embedded, axis=(0, 1)), jnp.sum(delta_embedded * normed, axis=(0, 1))),
        ("dp", "fsdp"),
    )
    visual_delta_rows = (
        valid_slot
        * back_batch_gain.astype(jnp.float32)
        * inverse_spread
        * (delta_embedded - shift_total / segment_total - normed * gain_total / segment_total)
    ).astype(jnp.bfloat16)
    visual_local = jnp.einsum(
        "bli,blz->iz", pooled_segments, visual_delta_rows, preferred_element_type=jnp.float32
    )
    delta_pooled = (
        jnp.einsum(
            "zbl,wl->zbw", visual_delta_rows, visual_pullback, preferred_element_type=jnp.float32
        )
        / divisor
    )
    text_gradient = delta_joined + jnp.einsum(
        "drs,dsc->drc",
        onehot_wide,
        delta_pooled,
        precision=highest_precision,
        preferred_element_type=jnp.float32,
    )
    (
        visual_shard,
        attend_shard,
        merge_shard,
        first_gain_shard,
        first_shift_shard,
        up_shard,
        down_shard,
        second_gain_shard,
        second_shift_shard,
    ) = (
        lax.psum_scatter(
            visual_local.astype(jnp.bfloat16), "fsdp", scatter_dimension=0, tiled=True
        ).astype(jnp.float32),
        lax.psum_scatter(
            attend_local.astype(jnp.bfloat16), "fsdp", scatter_dimension=0, tiled=True
        ).astype(jnp.float32),
        lax.psum_scatter(
            merge_local.astype(jnp.bfloat16), "fsdp", scatter_dimension=0, tiled=True
        ).astype(jnp.float32),
        lax.psum_scatter(
            first_gain_local.astype(jnp.bfloat16), "fsdp", scatter_dimension=0, tiled=True
        ).astype(jnp.float32),
        lax.psum_scatter(
            first_shift_local.astype(jnp.bfloat16), "fsdp", scatter_dimension=0, tiled=True
        ).astype(jnp.float32),
        lax.psum_scatter(
            up_local.astype(jnp.bfloat16), "fsdp", scatter_dimension=0, tiled=True
        ).astype(jnp.float32),
        lax.psum_scatter(
            down_local.astype(jnp.bfloat16), "fsdp", scatter_dimension=0, tiled=True
        ).astype(jnp.float32),
        lax.psum_scatter(
            second_gain_local.astype(jnp.bfloat16), "fsdp", scatter_dimension=0, tiled=True
        ).astype(jnp.float32),
        lax.psum_scatter(
            second_shift_local.astype(jnp.bfloat16), "fsdp", scatter_dimension=0, tiled=True
        ).astype(jnp.float32),
    )
    summed = (
        lax.psum(visual_shard.astype(jnp.bfloat16), "dp").astype(jnp.float32),
        lax.psum(attend_shard.astype(jnp.bfloat16), "dp").astype(jnp.float32),
        lax.psum(merge_shard.astype(jnp.bfloat16), "dp").astype(jnp.float32),
        lax.psum(first_gain_shard.astype(jnp.bfloat16), "dp").astype(jnp.float32),
        lax.psum(first_shift_shard.astype(jnp.bfloat16), "dp").astype(jnp.float32),
        lax.psum(up_shard.astype(jnp.bfloat16), "dp").astype(jnp.float32),
        lax.psum(down_shard.astype(jnp.bfloat16), "dp").astype(jnp.float32),
        lax.psum(second_gain_shard.astype(jnp.bfloat16), "dp").astype(jnp.float32),
        lax.psum(second_shift_shard.astype(jnp.bfloat16), "dp").astype(jnp.float32),
    )
    (
        visual_gradient,
        attend_gradient,
        merge_gradient,
        first_gain_gradient,
        first_shift_gradient,
        up_gradient,
        down_gradient,
        second_gain_gradient,
        second_shift_gradient,
    ) = summed
    piece = features // lax.axis_size("fsdp")
    start = lax.axis_index("fsdp") * piece
    batch_gain_gradient = lax.dynamic_slice_in_dim(gain_total, start, piece, 0)
    batch_shift_gradient = lax.dynamic_slice_in_dim(shift_total, start, piece, 0)
    return (
        layer_output,
        text_gradient,
        visual_gradient,
        batch_gain_gradient,
        batch_shift_gradient,
        attend_gradient,
        merge_gradient,
        first_gain_gradient,
        first_shift_gradient,
        up_gradient,
        down_gradient,
        second_gain_gradient,
        second_shift_gradient,
    )


def solution(mesh):
    in_specs = (
        P(("dp", "fsdp"), None, None),
        P("fsdp", None),
        P("fsdp"),
        P("fsdp"),
        P("fsdp", None),
        P("fsdp", None),
        P("fsdp"),
        P("fsdp"),
        P("fsdp", None),
        P("fsdp", None),
        P("fsdp"),
        P("fsdp"),
        P(("dp", "fsdp")),
        P(("dp", "fsdp"), None),
        P(("dp", "fsdp"), None),
        P(("dp", "fsdp"), None, None),
    )
    out_specs = (
        P(("dp", "fsdp"), None, None),
        P(("dp", "fsdp"), None, None),
        P("fsdp", None),
        P("fsdp"),
        P("fsdp"),
        P("fsdp", None),
        P("fsdp", None),
        P("fsdp"),
        P("fsdp"),
        P("fsdp", None),
        P("fsdp", None),
        P("fsdp"),
        P("fsdp"),
    )
    return jax.shard_map(shards, mesh=mesh, in_specs=in_specs, out_specs=out_specs, check_vma=False)
```

profile of v0, /device:TPU:0, one launch (start us, length us, event | category | flops | bytes accessed | tf_op | source)
XLA Modules:
  0.0 913.8 jit_solution(14838720792702939342)
XLA Ops:
  20.4 39.1 %all-reduce.13 = (bf16[768]{0:T(1024)(128)(2,1)S(1)}, bf16[768]{0:T(1024)(128)(2,1)S(1)}, bf16[768]{0:T(1024)(128)(2,1)S(1)}, bf16[768]{0:T(1024)(128)(2,1)S(1)}, bf16[768]{0:T(1024)(128)(2,1)S(1)}) all-reduce(bf16[768]{0:T(1024)(128)(2,1)S(1)} %dynamic-update-slice.1, ...), channel_id=1, replica_groups=mesh['dp'=4,'fsdp'=8] {'fsdp'}, use_global_device_ids=true, to_apply=%add.1 | all-reduce | flops 3840 | bytes 15360
  61.3 2.1 fusion.47
  63.5 2.0 multiply_reduce_fusion.6
  65.5 38.1 %all-reduce.11 = (f32[768]{0:T(1024)S(1)}, f32[]{:T(128)}) all-reduce(f32[768]{0:T(1024)S(1)} %get-tuple-element.172, f32[]{:T(128)S(6)} %convert_element_type.181), channel_id=1, replica_groups=mesh['dp'=4,'fsdp'=8] {'dp','fsdp'}, use_global_device_ids=true, to_apply=%region_2.0 | all-reduce | flops 769 | bytes 6152 | tf_op jit(solution)/shard_map/psum | solution.py:157
  104.5 42.7 %psum.100 = f32[768]{0:T(1024)S(1)} all-reduce(f32[768]{0:T(1024)S(1)} %fusion.53), channel_id=1, replica_groups=mesh['dp'=4,'fsdp'=8] {'dp','fsdp'}, use_global_device_ids=true, to_apply=%region_6.0 | all-reduce | flops 768 | bytes 6144 | tf_op jit(solution)/shard_map/psum | solution.py:163
  147.8 2.3 fusion.55
  150.1 9.0 convolution_convert_fusion
  159.1 6.8 copy.50
  165.9 22.8 %while.22 = (s32[]{:T(128)}, bf16[2,512,768]{1,2,0:T(8,128)(2,1)S(1)}, f32[2,12,512]{2,1,0:T(8,128)S(1)}, bf16[2,512,2304]{1,2,0:T(8,128)(2,1)}, s32[2,512]{1,0:T(2,128)S(1)}, /*index=5*/s32[]{:T(128)}) while((s32[]{:T(128)}, bf16[2,512,768]{1,2,0:T(8,128)(2,1)S(1)}, f32[2,12,512]{2,1,0:T(8,128)S(1)}, bf16[2,512,2304]{1,2,0:T(8,128)(2,1)}, ...), condition=%wide.region_10.11_spmd, body=%wide.region_7.10_spmd.sunk | while | flops 843442688 | bytes 52129876 | solution.py:177
  166.4 1.8 dynamic-slice_bitcast_fusion.6
  168.4 3.1 fusion.131
  171.5 2.6 fusion.132
  174.1 3.3 fusion.133
  177.5 1.8 dynamic-slice_bitcast_fusion.6
  179.5 3.1 fusion.131
  182.6 2.6 fusion.132
  185.2 3.3 fusion.133
  189.9 4.8 fusion.77
  195.2 48.8 %all-gather.12.cloned.1.call-done = bf16[768,3072]{1,0:T(8,128)(2,1)} async-done(((bf16[96,3072]{1,0:T(8,128)(2,1)}), bf16[768,3072]{1,0:T(8,128)(2,1)}) %all-gather.12.cloned.1.call-update) | async-done | bytes 4718608 | tf_op jit(solution)/shard_map/all_gather | solution.py:124
  244.0 14.9 %fusion.36 = (u8[512,3072]{1,0:T(8,128)(4,1)S(1)}, u8[512,3072]{1,0:T(8,128)(4,1)S(1)}, f32[2,512,3072]{2,1,0:T(8,128)}) fusion(bf16[768,3072]{1,0:T(8,128)(2,1)} %all-gather.12.cloned.1.call-done, f32[2,512,768]{2,1,0:T(8,128)S(1)} %get-tuple-element.175, f32[768]{0:T(1024)S(1)} %copy-done.50, f32[768]{0:T(1024)S(1)} %copy-done.40, ...), kind=kOutput, calls=%fused_computation.80 | convolution fusion | flops 4873519104 | bytes 23607296 | tf_op jit(solution)/shard_map/sjq,qy->sjy/dot_general | solution.py:184
  258.9 31.0 %multiply_convert_fusion.3 = (bf16[2,512,3072]{2,1,0:T(8,128)(2,1)}, f32[2,512,3072]{2,1,0:T(8,128)}) fusion(f32[2,512,3072]{2,1,0:T(8,128)} %get-tuple-element.176, u8[512,3072]{1,0:T(8,128)(4,1)S(1)} %get-tuple-element.99, u8[512,3072]{1,0:T(8,128)(4,1)S(1)} %get-tuple-element.98), kind=kLoop, calls=%fused_computation.37 | loop fusion | flops 220200960 | bytes 34603008 | tf_op jit(solution)/shard_map/convert_element_type | solution.py:190
  289.9 34.1 %all-gather.14.cloned.1.call-done = bf16[3072,768]{1,0:T(8,128)(2,1)} async-done(((bf16[384,768]{1,0:T(8,128)(2,1)}), bf16[3072,768]{1,0:T(8,128)(2,1)}) %all-gather.14.cloned.1.call-update) | async-done | bytes 4718608 | tf_op jit(solution)/shard_map/all_gather | solution.py:125
  324.1 9.5 %fusion.78 = (f32[2,512]{1,0:T(2,128)S(1)}, f32[2,512,768]{2,1,0:T(8,128)S(1)}) fusion(bf16[2,512,3072]{2,1,0:T(8,128)(2,1)} %get-tuple-element.156, bf16[3072,768]{1,0:T(8,128)(2,1)} %all-gather.14.cloned.1.call-done, f32[768]{0:T(1024)S(1)} %copy-done.50, f32[768]{0:T(1024)S(1)} %copy-done.40, f32[2,512]{1,0:T(2,128)S(1)} %fusion.66, ...), kind=kOutput, calls=%fused_computation.142 | convolution fusion | flops 4836555776 | bytes 17319936 | tf_op jit(solution)/shard_map/zya,av->zyv/dot_general | solution.py:191
  334.7 2.4 fusion.34
  337.1 16.4 %add_convert_fusion = bf16[2,512,3072]{2,1,0:T(8,128)(2,1)} fusion(f32[2,512,3072]{2,1,0:T(8,128)} %get-tuple-element.157, f32[2,512,3072]{2,1,0:T(8,128)} %get-tuple-element.176, bf16[3072,768]{1,0:T(8,128)(2,1)} %all-gather.14.cloned.1.call-done, f32[2,512]{1,0:T(2,128)S(1)} %negate_multiply_fusion.2, bf16[2,512,768]{2,1,0:T(8,128)(2,1)} %param.35, ...), kind=kOutput, calls=%fused_computation.36 | convolution fusion | flops 4882956288 | bytes 40913920 | tf_op jit(solution)/shard_map/ivj,hj->ivh/dot_general | solution.py:229
  353.5 11.2 %multiply_reduce_fusion.1 = (bf16[768]{0:T(1024)(128)(2,1)}, f32[2,512]{1,0:T(2,128)S(1)}, bf16[768]{0:T(1024)(128)(2,1)}, f32[2,512,768]{2,1,0:T(8,128)S(1)}) fusion(f32[2,512,768]{2,1,0:T(8,128)} %copy-done.2, f32[2,512]{1,0:T(2,128)S(1)} %fusion.66, f32[2,512]{1,0:T(2,128)S(1)} %broadcast_multiply_fusion.1, f32[768]{0:T(1024)S(1)} %copy-done.40, ...), kind=kOutput, calls=%fused_computation.72 | convolution fusion | flops 4845204480 | bytes 22057984 | tf_op jit(solution)/shard_map/wmx,ix->wmi/dot_general | solution.py:237
  366.1 2.5 bitcast_convert_fusion.3
  368.8 3.9 convolution_convert_fusion.1
  372.6 77.6 %while.23 = (s32[]{:T(128)}, bf16[2,512,2304]{1,2,0:T(8,128)(2,1)}, bf16[2,512,2304]{1,2,0:T(8,128)(2,1)}, s32[2,512]{1,0:T(2,128)S(1)}, f32[2,12,512]{2,1,0:T(8...) while((s32[]{:T(128)}, bf16[2,512,2304]{1,2,0:T(8,128)(2,1)}, bf16[2,512,2304]{1,2,0:T(8,128)(2,1)}, ...), condition=%wide.region_21.22_spmd, body=%wide.region_19.21_spmd.sunk | while | flops 2069490176 | bytes 163754704 | solution.py:254
  373.0 1.9 dynamic-slice_bitcast_fusion.7
  375.1 6.4 fusion.145
  383.9 11.5 %multiply_reduce_fusion.8 = (f32[12,512]{1,0:T(8,128)S(1)}, f32[12,512,512]{1,2,0:T(8,128)}) fusion(f32[12,512,512]{1,2,0:T(8,128)} %fusion.145, f32[12,512]{1,0:T(8,128)S(1)} %dynamic-slice_bitcast_fusion.8, pred[512]{0:T(512)(128)(4,1)S(1)} %compare_reduce_fusion.5, bf16[512,12,64]{0,2,1:T(8,128)(2,1)S(1)} %bitcast.169, ...), kind=kOutput, calls=%fused_computation.14.clone.1 | convolution fusion | flops 418375680 | bytes 26788352 | tf_op jit(solution)/shard_map/while/body/eval_jaxpr/qhe,khe->hqk/dot_general | solution.py:67
  396.7 7.1 multiply_convert_fusion.8
  405.0 2.0 multiply_convert_fusion.9
  407.0 3.1 fusion.146
  410.0 1.6 maximum_dynamic-update-slice_fusion.2
  411.6 1.8 dynamic-slice_bitcast_fusion.7
  413.6 6.4 fusion.145
  422.4 11.5 %multiply_reduce_fusion.8 = (f32[12,512]{1,0:T(8,128)S(1)}, f32[12,512,512]{1,2,0:T(8,128)}) fusion(f32[12,512,512]{1,2,0:T(8,128)} %fusion.145, f32[12,512]{1,0:T(8,128)S(1)} %dynamic-slice_bitcast_fusion.8, pred[512]{0:T(512)(128)(4,1)S(1)} %compare_reduce_fusion.5, bf16[512,12,64]{0,2,1:T(8,128)(2,1)S(1)} %bitcast.169, ...), kind=kOutput, calls=%fused_computation.14.clone.1 | convolution fusion | flops 418375680 | bytes 26788352 | tf_op jit(solution)/shard_map/while/body/eval_jaxpr/qhe,khe->hqk/dot_general | solution.py:67
  435.1 7.1 multiply_convert_fusion.8
  443.3 2.0 multiply_convert_fusion.9
  445.3 3.1 fusion.146
  448.4 1.6 maximum_dynamic-update-slice_fusion.2
  450.3 8.5 add_add_fusion.2
  458.8 1.6 copy-done.8
  460.4 1.5 fusion.71
  461.9 38.4 %all-reduce.10 = (f32[768]{0:T(1024)S(1)}, f32[768]{0:T(1024)S(1)}) all-reduce(f32[768]{0:T(1024)S(1)} %get-tuple-element.108, f32[768]{0:T(1024)S(1)} %get-tuple-element.107), channel_id=1, replica_groups=mesh['dp'=4,'fsdp'=8] {'dp','fsdp'}, use_global_device_ids=true, to_apply=%region_25.26 | all-reduce | flops 1536 | bytes 12288 | tf_op jit(solution)/shard_map/psum | solution.py:268
  502.7 1.5 bitcast_convert_fusion.4
  505.0 8.5 bitcast_convert_fusion.2
  513.8 1.6 copy-done.1
  515.4 11.2 %bitcast_convert_fusion = bf16[3072,768]{1,0:T(8,128)(2,1)} fusion(bf16[2,512,3072]{2,1,0:T(8,128)(2,1)} %get-tuple-element.156, f32[2,512]{1,0:T(2,128)S(1)} %copy-done.53, bf16[2,512,768]{2,1,0:T(8,128)(2,1)} %param.35, f32[2,512,768]{2,1,0:T(8,128)S(1)} %copy-done.1, f32[2,512]{1,0:T(2,128)S(1)} %copy-done.46, f32[768]{0:T(1024)S(1)} %copy-done.27, ...), kind=kOutput, calls=%fused_computation.50 | convolution fusion | flops 4841275392 | bytes 15748096 | tf_op jit(solution)/shard_map/omt,oms->ts/dot_general | solution.py:226
  527.3 10.5 %bitcast_convert_fusion.1 = bf16[768,3072]{1,0:T(8,128)(2,1)} fusion(bf16[2,512,3072]{2,1,0:T(8,128)(2,1)} %add_convert_fusion, f32[2,512,768]{2,1,0:T(8,128)} %copy-done.2, f32[768]{0:T(1024)S(1)} %copy-done.51, f32[768]{0:T(1024)S(1)} %copy-done.41, f32[2,512]{1,0:T(2,128)S(1)} %copy-done.43, f32[2,512]{1,0:T(2,128)S(1)} %copy-done.37), kind=kOutput, calls=%fused_computation.51 | convolution fusion | flops 4838129664 | bytes 14170112 | tf_op jit(solution)/shard_map/oih,oiu->hu/dot_general | solution.py:234
  537.9 2.3 reduce_sum.212
  545.3 37.0 %all-reduce.12 = (bf16[768]{0:T(1024)(128)(2,1)}, bf16[768]{0:T(1024)(128)(2,1)}, bf16[768]{0:T(1024)(128)(2,1)}, bf16[768]{0:T(1024)(128)(2,1)}, bf16[768]{0:T(1024)(128)(2,1)}) all-reduce(bf16[768]{0:T(1024)(128)(2,1)} %dynamic-update-slice.5, bf16[768]{0:T(1024)(128)(2,1)} %get-tuple-element.100, ...), channel_id=1, replica_groups=mesh['dp'=4,'fsdp'=8] {'fsdp'}, use_global_device_ids=true, to_apply=%add.5 | all-reduce | flops 3840 | bytes 15360
  587.4 6.9 all-reduce.14
  600.3 50.8 %reduce-scatter.8.cloned.1.call-done = bf16[96,2304]{1,0:T(8,128)(2,1)} async-done(((bf16[768,2304]{1,0:T(8,128)(2,1)}), bf16[96,2304]{1,0:T(8,128)(2,1)}) %reduce-scatter.8.cloned.1.call-update) | async-done | bytes 442384 | tf_op jit(solution)/shard_map/reduce_scatter | solution.py:308
  651.0 98.7 %reduce-scatter.14.cloned.1.call-done = bf16[384,768]{1,0:T(8,128)(2,1)} async-done(((bf16[3072,768]{1,0:T(8,128)(2,1)}), bf16[384,768]{1,0:T(8,128)(2,1)}) %reduce-scatter.14.cloned.1.call-update) | async-done | bytes 589840 | tf_op jit(solution)/shard_map/reduce_scatter | solution.py:323
  749.7 98.5 %reduce-scatter.12.cloned.1.call-done = bf16[96,3072]{1,0:T(8,128)(2,1)} async-done(((bf16[768,3072]{1,0:T(8,128)(2,1)}), bf16[96,3072]{1,0:T(8,128)(2,1)}) %reduce-scatter.12.cloned.1.call-update) | async-done | bytes 589840 | tf_op jit(solution)/shard_map/reduce_scatter | solution.py:320
  848.3 1.8 convolution_divide_fusion
  850.1 2.2 multiply_add_fusion
  853.0 3.2 convolution_add_fusion
  856.2 44.0 %all-reduce.18.cloned.1.call-done = (bf16[96,768]{1,0:T(8,128)(2,1)}, bf16[96,2304]{1,0:T(8,128)(2,1)}, bf16[96,768]{1,0:T(8,128)(2,1)}, bf16[96,3072]{1,0:T(8,128)(2,1)}, bf16[384,768]{1,0:T(8,128)(2,1)}) async-done(((bf16[96,768]{1,0:T(8,128)(2,1)}, bf16[96,2304]{1,0:T(8,128)(2,1)}, bf16[96,768]{1,0:T(8,128)(2,1)}, bf16[96,3072]{1,0:T(8,128)(2,1)}, bf16[384,768]{1,0:T(8,128)(2,1)}), ...) | async-done | bytes 1916944 | tf_op jit(solution)/shard_map/psum | solution.py:334
  900.2 2.2 convert_element_type.210
  902.4 2.2 convert_element_type.212
  (231 shorter events, 52.4 us)
Async XLA Ops:
  7.2 56.3 %all-gather.6.cloned.1.call-start = ((), (), s32[]{:S(2)}) async-start(), calls=%async_computation.5 | async-start | bytes 1327104 | tf_op jit(solution)/shard_map/all_gather | solution.py:117
  7.9 142.2 %all-gather.8.cloned.1.call-start = ((), (), s32[]{:S(2)}) async-start(), calls=%async_computation.6 | async-start | bytes 3981312 | tf_op jit(solution)/shard_map/all_gather | solution.py:120
  8.7 180.1 %all-gather.10.cloned.1.call-start = ((), (), s32[]{:S(2)}) async-start(), calls=%async_computation.7 | async-start | bytes 1327104 | tf_op jit(solution)/shard_map/all_gather | solution.py:121
  9.4 234.6 %all-gather.12.cloned.1.call-start = ((), (), s32[]{:S(2)}) async-start(), calls=%async_computation.8 | async-start | bytes 5308416 | tf_op jit(solution)/shard_map/all_gather | solution.py:124
  10.0 314.1 %all-gather.14.cloned.1.call-start = ((), (), s32[]{:S(2)}) async-start(), calls=%async_computation.9 | async-start | bytes 5308416 | tf_op jit(solution)/shard_map/all_gather | solution.py:125
  10.6 589.7 %reduce-scatter.10.cloned.1.call-start = ((), (), s32[]{:S(2)}) async-start(), calls=%async_computation.12 | async-start | bytes 1327104 | tf_op jit(solution)/shard_map/reduce_scatter | solution.py:311
  11.4 92.9 %copy-start.47 = (f32[2,128]{1,0:T(2,128)}, f32[2,128]{1,0:T(2,128)S(1)}, u32[]{:S(2)}) copy-start(f32[2,128]{1,0:T(2,128)S(1)} %compare_convert_fusion) | copy-start | bytes 3076
  13.6 49.9 %copy-start.57 = (f32[2,128]{1,0:T(2,128)}, f32[2,128]{1,0:T(2,128)S(1)}, u32[]{:S(2)}) copy-start(f32[2,128]{1,0:T(2,128)S(1)} %broadcast_maximum_fusion) | copy-start | bytes 3076
  59.5 88.3 %copy-start.34 = (f32[768]{0:T(1024)}, f32[768]{0:T(1024)S(1)}, u32[]{:S(2)}) copy-start(f32[768]{0:T(1024)S(1)} %convert_element_type.182) | copy-start | bytes 9220
  61.3 86.5 %copy-start.30 = (s32[2,512]{1,0:T(2,128)S(1)}, s32[2,512]{1,0:T(2,128)}, u32[]{:S(2)}) copy-start(s32[2,512]{1,0:T(2,128)} %param.33) | copy-start | bytes 12292
  63.4 86.7 %copy-start.16 = (bf16[2,128,768]{2,1,0:T(8,128)(2,1)}, bf16[2,128,768]{2,1,0:T(8,128)(2,1)S(1)}, u32[]{:S(2)}) copy-start(bf16[2,128,768]{2,1,0:T(8,128)(2,1)S(1)} %fusion.47) | copy-start | bytes 1179652
  63.5 86.7 %copy-start.12 = (bf16[2,512,768]{2,1,0:T(8,128)(2,1)S(1)}, bf16[2,512,768]{2,1,0:T(8,128)(2,1)}, u32[]{:S(2)}) copy-start(bf16[2,512,768]{2,1,0:T(8,128)(2,1)} %param.20) | copy-start | bytes 4718596
  65.5 93.5 %copy-start.4 = (f32[2,128,768]{2,1,0:T(8,128)}, f32[2,128,768]{2,1,0:T(8,128)S(1)}, u32[]{:S(2)}) copy-start(f32[2,128,768]{2,1,0:T(8,128)S(1)} %get-tuple-element.173) | copy-start | bytes 2359300
  104.3 54.8 %copy-start.24 = (f32[768]{0:T(1024)}, f32[768]{0:T(1024)S(1)}, u32[]{:S(2)}) copy-start(f32[768]{0:T(1024)S(1)} %broadcast_divide_fusion.1) | copy-start | bytes 9220
  147.8 11.3 %copy-start.32 = (f32[768]{0:T(1024)}, f32[768]{0:T(1024)S(1)}, u32[]{:S(2)}) copy-start(f32[768]{0:T(1024)S(1)} %add_rsqrt_fusion) | copy-start | bytes 9220
  159.1 6.8 copy-start.13
  159.1 6.8 copy-start.23
  194.6 64.2 %copy-start.2 = (f32[2,512,768]{2,1,0:T(8,128)}, f32[2,512,768]{2,1,0:T(8,128)S(1)}, u32[]{:S(2)}) copy-start(f32[2,512,768]{2,1,0:T(8,128)S(1)} %get-tuple-element.175) | copy-start | bytes 9437188
  194.6 49.3 %copy-start.40 = (f32[768]{0:T(1024)S(1)}, f32[768]{0:T(1024)}, u32[]{:S(2)}) copy-start(f32[768]{0:T(1024)} %convert_element_type.187) | copy-start | bytes 9220
  194.7 49.3 %copy-start.50 = (f32[768]{0:T(1024)S(1)}, f32[768]{0:T(1024)}, u32[]{:S(2)}) copy-start(f32[768]{0:T(1024)} %convert_element_type.188) | copy-start | bytes 9220
  194.7 170.0 %copy-start.36 = (f32[2,512]{1,0:T(2,128)}, f32[2,512]{1,0:T(2,128)S(1)}, u32[]{:S(2)}) copy-start(f32[2,512]{1,0:T(2,128)S(1)} %broadcast_multiply_fusion.1) | copy-start | bytes 12292
  195.2 169.5 %copy-start.42 = (f32[2,512]{1,0:T(2,128)}, f32[2,512]{1,0:T(2,128)S(1)}, u32[]{:S(2)}) copy-start(f32[2,512]{1,0:T(2,128)S(1)} %fusion.66) | copy-start | bytes 12292
  324.1 9.6 %copy-start.6 = (bf16[2,512,768]{2,1,0:T(8,128)(2,1)S(1)}, bf16[2,512,768]{2,1,0:T(8,128)(2,1)}, u32[]{:S(2)}) copy-start(bf16[2,512,768]{2,1,0:T(8,128)(2,1)} %param.35) | copy-start | bytes 4718596
  324.1 9.6 %copy-start.26 = (f32[768]{0:T(1024)S(1)}, f32[768]{0:T(1024)}, u32[]{:S(2)}) copy-start(f32[768]{0:T(1024)} %convert_element_type.191) | copy-start | bytes 9220
  333.6 19.8 %copy-start = (f32[2,512,768]{2,1,0:T(8,128)}, f32[2,512,768]{2,1,0:T(8,128)S(1)}, u32[]{:S(2)}) copy-start(f32[2,512,768]{2,1,0:T(8,128)S(1)} %get-tuple-element.178) | copy-start | bytes 9437188
  333.6 19.8 %copy-start.28 = (f32[2,512]{1,0:T(2,128)}, f32[2,512]{1,0:T(2,128)S(1)}, u32[]{:S(2)}) copy-start(f32[2,512]{1,0:T(2,128)S(1)} %broadcast_multiply_fusion) | copy-start | bytes 12292
  334.7 18.8 %copy-start.38 = (f32[2,512]{1,0:T(2,128)}, f32[2,512]{1,0:T(2,128)S(1)}, u32[]{:S(2)}) copy-start(f32[2,512]{1,0:T(2,128)S(1)} %get-tuple-element.169) | copy-start | bytes 12292
  334.7 18.8 %copy-start.45 = (f32[2,512]{1,0:T(2,128)}, f32[2,512]{1,0:T(2,128)S(1)}, u32[]{:S(2)}) copy-start(f32[2,512]{1,0:T(2,128)S(1)} %get-tuple-element.168) | copy-start | bytes 12292
  337.1 16.4 %copy-start.52 = (f32[2,512]{1,0:T(2,128)}, f32[2,512]{1,0:T(2,128)S(1)}, u32[]{:S(2)}) copy-start(f32[2,512]{1,0:T(2,128)S(1)} %negate_multiply_fusion.2) | copy-start | bytes 12292
  353.5 11.2 %copy-start.3 = (f32[2,512,768]{2,1,0:T(8,128)S(1)}, f32[2,512,768]{2,1,0:T(8,128)}, u32[]{:S(2)}) copy-start(f32[2,512,768]{2,1,0:T(8,128)} %copy-done.2) | copy-start | bytes 9437188
  365.9 2.8 copy-start.11
  366.0 2.8 copy-start.55
  368.7 231.6 %reduce-scatter.6.cloned.1.call-start = ((), (), s32[]{:S(2)}) async-start(), calls=%async_computation.10 | async-start | bytes 1327104 | tf_op jit(solution)/shard_map/reduce_scatter | solution.py:305
  372.6 77.6 %copy-start.56 = (f32[2,512]{1,0:T(2,128)S(1)}, f32[2,512]{1,0:T(2,128)}, u32[]{:S(2)}) copy-start(f32[2,512]{1,0:T(2,128)} %copy-done.55) | copy-start | bytes 12292
  375.1 6.4 copy-start.10
  383.9 11.6 %slice-start = ((s8[12582912]{0:T(1024)(128)(4,1)}), s8[4194304]{0:T(1024)(128)(4,1)S(1)}, s32[]{:S(2)}) async-start(s8[12582912]{0:T(1024)(128)(4,1)} %bitcast.161), calls=%async_computation.16 | async-start | bytes 8388608 | tf_op jit(solution)/shard_map/while
  383.9 11.5 %slice-start.1 = ((s8[12582912]{0:T(1024)(128)(4,1)}), s8[4194304]{0:T(1024)(128)(4,1)S(1)}, s32[]{:S(2)}) async-start(s8[12582912]{0:T(1024)(128)(4,1)} %bitcast.161), calls=%async_computation.17 | async-start | bytes 8388608 | tf_op jit(solution)/shard_map/while
  383.9 12.8 %slice-start.2 = ((s8[12582912]{0:T(1024)(128)(4,1)}), s8[4194304]{0:T(1024)(128)(4,1)S(1)}, s32[]{:S(2)}) async-start(s8[12582912]{0:T(1024)(128)(4,1)} %bitcast.161), calls=%async_computation.18 | async-start | bytes 8388608 | tf_op jit(solution)/shard_map/while
  413.6 6.4 copy-start.10
  422.4 11.5 %slice-start = ((s8[12582912]{0:T(1024)(128)(4,1)}), s8[4194304]{0:T(1024)(128)(4,1)S(1)}, s32[]{:S(2)}) async-start(s8[12582912]{0:T(1024)(128)(4,1)} %bitcast.161), calls=%async_computation.16 | async-start | bytes 8388608 | tf_op jit(solution)/shard_map/while
  422.4 11.5 %slice-start.1 = ((s8[12582912]{0:T(1024)(128)(4,1)}), s8[4194304]{0:T(1024)(128)(4,1)S(1)}, s32[]{:S(2)}) async-start(s8[12582912]{0:T(1024)(128)(4,1)} %bitcast.161), calls=%async_computation.17 | async-start | bytes 8388608 | tf_op jit(solution)/shard_map/while
  422.4 12.7 %slice-start.2 = ((s8[12582912]{0:T(1024)(128)(4,1)}), s8[4194304]{0:T(1024)(128)(4,1)S(1)}, s32[]{:S(2)}) async-start(s8[12582912]{0:T(1024)(128)(4,1)} %bitcast.161), calls=%async_computation.18 | async-start | bytes 8388608 | tf_op jit(solution)/shard_map/while
  450.2 10.2 %copy-start.5 = (f32[2,128,768]{2,1,0:T(8,128)S(1)}, f32[2,128,768]{2,1,0:T(8,128)}, u32[]{:S(2)}) copy-start(f32[2,128,768]{2,1,0:T(8,128)} %copy-done.4) | copy-start | bytes 2359300
  450.2 10.2 %copy-start.25 = (f32[768]{0:T(1024)S(1)}, f32[768]{0:T(1024)}, u32[]{:S(2)}) copy-start(f32[768]{0:T(1024)} %copy-done.24) | copy-start | bytes 9220
  450.2 10.2 %copy-start.31 = (s32[2,512]{1,0:T(2,128)S(1)}, s32[2,512]{1,0:T(2,128)}, u32[]{:S(2)}) copy-start(s32[2,512]{1,0:T(2,128)} %param.33) | copy-start | bytes 12292
  450.2 10.1 %copy-start.33 = (f32[768]{0:T(1024)S(1)}, f32[768]{0:T(1024)}, u32[]{:S(2)}) copy-start(f32[768]{0:T(1024)} %copy-done.32) | copy-start | bytes 9220
  460.4 40.6 %copy-start.35 = (f32[768]{0:T(1024)S(1)}, f32[768]{0:T(1024)}, u32[]{:S(2)}) copy-start(f32[768]{0:T(1024)} %copy-done.34) | copy-start | bytes 9220
  460.4 40.6 %copy-start.48 = (f32[2,128]{1,0:T(2,128)S(1)}, f32[2,128]{1,0:T(2,128)}, u32[]{:S(2)}) copy-start(f32[2,128]{1,0:T(2,128)} %copy-done.47) | copy-start | bytes 3076
  460.4 42.3 %copy-start.17 = (bf16[2,128,768]{2,1,0:T(8,128)(2,1)S(1)}, bf16[2,128,768]{2,1,0:T(8,128)(2,1)}, u32[]{:S(2)}) copy-start(bf16[2,128,768]{2,1,0:T(8,128)(2,1)} %copy-done.16) | copy-start | bytes 1179652
  502.7 2.3 copy-start.7
  504.3 146.8 %reduce-scatter.8.cloned.1.call-start = ((), (), s32[]{:S(2)}) async-start(), calls=%async_computation.11 | async-start | bytes 3981312 | tf_op jit(solution)/shard_map/reduce_scatter | solution.py:308
  513.5 1.9 copy-start.1
  513.5 1.9 copy-start.27
  513.5 1.9 copy-start.29
  513.5 1.9 copy-start.39
  513.5 1.9 copy-start.46
  513.6 236.1 %reduce-scatter.14.cloned.1.call-start = ((), (), s32[]{:S(2)}) async-start(), calls=%async_computation.14 | async-start | bytes 5308416 | tf_op jit(solution)/shard_map/reduce_scatter | solution.py:323
  526.6 321.6 %reduce-scatter.12.cloned.1.call-start = ((), (), s32[]{:S(2)}) async-start(), calls=%async_computation.13 | async-start | bytes 5308416 | tf_op jit(solution)/shard_map/reduce_scatter | solution.py:320
  537.8 310.5 %copy-start.19 = (bf16[2,128,768]{2,1,0:T(8,128)(2,1)S(1)}, bf16[2,128,768]{2,1,0:T(8,128)(2,1)}, u32[]{:S(2)}) copy-start(bf16[2,128,768]{2,1,0:T(8,128)(2,1)} %copy-done.18) | copy-start | bytes 1179652
  537.8 362.3 %all-reduce.18.cloned.1.call-start = ((), (), s32[]{:S(2)}) async-start(), calls=%async_computation.15 | async-start | bytes 3833856 | tf_op jit(solution)/shard_map/psum | solution.py:334
  850.1 2.9 copy-start.9
  900.2 4.4 copy-start.20
  900.2 5.4 copy-start.22
  900.2 6.1 copy-start.21
  (12 other events, 12.7 us)
Sparse Core Ops, SparseCore 0:
  10.2 44.0 all-gather.5
  56.5 64.8 all-gather.7
  123.5 39.6 all-gather.9
  165.3 78.6 all-gather.11
  246.0 78.0 all-gather.13
  368.8 62.2 reduce-scatter.9
  504.4 64.7 reduce-scatter.5
  572.9 78.1 reduce-scatter.7
  654.7 94.9 reduce-scatter.13
  753.2 95.0 reduce-scatter.11
  851.0 49.1 all-reduce.17
where the time goes:
time: 922 us; the launch traced here: 914 us
  waiting for transfers between devices  378 us (41%)
  blocking collectives  202 us (22%)
  matrix products  186 us (20%)
  other arithmetic  84 us (9%)
  local copies, waits for them, and re-layouts  44.5 us (5%)
  between operations  16.8 us (2%)
    reduce_scatter x1, waiting for transfers between devices, shards(): lax.psum_scatter(down_local.astype(jnp.bfloat16), 'fsdp', scatter_dimensi...  98.7 us
    reduce_scatter x1, waiting for transfers between devices, shards(): lax.psum_scatter(up_local.astype(jnp.bfloat16), 'fsdp', scatter_dimension...  98.5 us
    unnamed x2, blocking collectives  76.1 us
    reduce_scatter x1, waiting for transfers between devices, shards(): lax.psum_scatter(attend_local.astype(jnp.bfloat16), 'fsdp', scatter_dimen...  50.8 us
    all_gather x1, waiting for transfers between devices, shards(): lax.all_gather(up_matrix, 'fsdp', axis=0, tiled=True)  48.8 us
    psum x1, waiting for transfers between devices, shards(): lax.psum(visual_shard.astype(jnp.bfloat16), 'dp').astype(jnp.float32)  44 us
    psum x1, blocking collectives, shards(): lax.psum(jnp.sum(valid_slot * center * center, axis=(0, 1)), ('dp', 'fsdp'))  42.7 us
    psum x1, blocking collectives, shards(): lax.psum((jnp.sum(delta_embedded, axis=(0, 1)), jnp.sum(delta_embedded *...  38.4 us
  transfers between devices with their start and end apart: 11, of which 6 were waited for; matrix products, arithmetic and copies ran while one was open for 28% of the time, Pallas kernels for 0%

commit v1 on v0

--- a/solution.py
+++ b/solution.py
@@ -9,6 +9,19 @@
 eps_batch = 1e-05
 masked_score = -1e30
 highest_precision = lax.Precision.HIGHEST
+
+
+def ring_gather(x, axis, dim):
+    peers, place, rows = (lax.axis_size(axis), lax.axis_index(axis), x.shape[dim])
+    forward = [(i, (i + 1) % peers) for i in range(peers)]
+    out = jnp.zeros((*x.shape[:dim], peers * rows, *x.shape[dim + 1 :]), x.dtype)
+    current = x
+    for hop in range(peers):
+        holder = (place - hop) % peers
+        out = lax.dynamic_update_slice_in_dim(out, current, holder * rows, axis=dim)
+        if hop < peers - 1:
+            current = lax.ppermute(current, axis, forward)
+    return out
 
 
 def layer_norm(values, gain, shift):
@@ -121,7 +134,7 @@
         lax.all_gather(merge_weight, "fsdp", axis=0, tiled=True),
         lax.all_gather(first_gain, "fsdp", axis=0, tiled=True),
         lax.all_gather(first_shift, "fsdp", axis=0, tiled=True),
-        lax.all_gather(up_matrix, "fsdp", axis=0, tiled=True),
+        ring_gather(up_matrix, "fsdp", 0),
         lax.all_gather(down_matrix, "fsdp", axis=0, tiled=True),
         lax.all_gather(second_gain, "fsdp", axis=0, tiled=True),
         lax.all_gather(second_shift, "fsdp", axis=0, tiled=True),

time: 922 us -> 973 us (1.055)
  blocking collectives: 202 us -> 235 us
    ppermute x0 -> x7, waiting for transfers between devices: none -> 83.5 us  [ring_gather(): current = lax.ppermute(current, axis, forward)]
    all_gather x1, waiting for transfers between devices: 48.8 us -> 0.01 us  [shards(): lax.all_gather(up_matrix, 'fsdp', axis=0, tiled=True)]
    all_gather x1, waiting for transfers between devices: 34.1 us -> 0.02 us  [shards(): lax.all_gather(down_matrix, 'fsdp', axis=0, tiled=True)]
    psum x1, blocking collectives: 38.1 us -> 55.3 us  [shards(): lax.psum((local_count, jnp.sum(masked_visual, axis=(0, 1))), ('dp', 'fsdp'))]
    unnamed x131 -> x137, local copies, waits for them, and re-layouts: 19.9 us -> 14.2 us
  transfers between devices with their start and end apart: 11 -> 18, of which waited for: 6 -> 8; matrix products, arithmetic and copies ran while one was open for 28% -> 30% of each run, Pallas kernels for 0% -> 0%
where the time goes in v1:
time: 973 us; the launch traced here: 965 us
  waiting for transfers between devices  378 us (39%)
  blocking collectives  235 us (24%)
  matrix products  188 us (19%)
  other arithmetic  85.2 us (9%)
  local copies, waits for them, and re-layouts  50.8 us (5%)
  between operations  17.1 us (2%)
    reduce_scatter x1, waiting for transfers between devices, shards(): lax.psum_scatter(up_local.astype(jnp.bfloat16), 'fsdp', scatter_dimension...  98.5 us
    reduce_scatter x1, waiting for transfers between devices, shards(): lax.psum_scatter(down_local.astype(jnp.bfloat16), 'fsdp', scatter_dimensi...  98.5 us
    ppermute x7, waiting for transfers between devices, ring_gather(): current = lax.ppermute(current, axis, forward)  83.5 us
    unnamed x2, blocking collectives  78.7 us
    psum x1, blocking collectives, shards(): lax.psum((local_count, jnp.sum(masked_visual, axis=(0, 1))), ('dp', 'fsdp'))  55.3 us
    reduce_scatter x1, waiting for transfers between devices, shards(): lax.psum_scatter(attend_local.astype(jnp.bfloat16), 'fsdp', scatter_dimen...  50.9 us
    psum x1, blocking collectives, shards(): lax.psum(jnp.sum(valid_slot * center * center, axis=(0, 1)), ('dp', 'fsdp'))  47.5 us
    psum x1, blocking collectives, shards(): lax.psum((jnp.sum(delta_embedded, axis=(0, 1)), jnp.sum(delta_embedded *...  46.9 us
  transfers between devices with their start and end apart: 18, of which 8 were waited for; matrix products, arithmetic and copies ran while one was open for 30% of the time, Pallas kernels for 0%

profile of v1, /device:TPU:0, one launch (start us, length us, event | category | flops | bytes accessed | tf_op | source)
XLA Modules:
  0.0 964.6 jit_solution(13696947852927896498)
XLA Ops:
  10.1 3.0 collective-permute-start
  14.1 19.1 %collective-permute-done = bf16[96,3072]{1,0:T(8,128)(2,1)S(1)} collective-permute-done((bf16[96,3072]{1,0:T(8,128)(2,1)}, bf16[96,3072]{1,0:T(8,128)(2,1)S(1)}, u32[]{:S(2)}, u32[]{:S(2)}) %collective-permute-start) | collective-permute-done | bytes 589856 | tf_op jit(solution)/shard_map/ppermute | solution.py:23
  33.3 2.0 fusion.47
  39.3 41.4 %all-reduce.13 = (bf16[768]{0:T(1024)(128)(2,1)S(1)}, bf16[768]{0:T(1024)(128)(2,1)S(1)}, bf16[768]{0:T(1024)(128)(2,1)S(1)}, bf16[768]{0:T(1024)(128)(2,1)S(1)}, bf16[768]{0:T(1024)(128)(2,1)S(1)}) all-reduce(bf16[768]{0:T(1024)(128)(2,1)S(1)} %dynamic-update-slice.1, ...), channel_id=1, replica_groups=mesh['dp'=4,'fsdp'=8] {'fsdp'}, use_global_device_ids=true, to_apply=%add.1 | all-reduce | flops 3840 | bytes 15360
  83.0 2.7 broadcast_in_dim.46
  88.7 14.5 %collective-permute-done.2 = bf16[96,3072]{1,0:T(8,128)(2,1)S(1)} collective-permute-done((bf16[96,3072]{1,0:T(8,128)(2,1)S(1)}, bf16[96,3072]{1,0:T(8,128)(2,1)S(1)}, u32[]{:S(2)}, u32[]{:S(2)}) %collective-permute-start.2) | collective-permute-done | bytes 589856 | tf_op jit(solution)/shard_map/ppermute | solution.py:23
  105.9 55.3 %all-reduce.11 = (f32[768]{0:T(1024)S(1)}, f32[]{:T(128)}) all-reduce(f32[768]{0:T(1024)S(1)} %get-tuple-element.172, f32[]{:T(128)S(6)} %convert_element_type.181), channel_id=1, replica_groups=mesh['dp'=4,'fsdp'=8] {'dp','fsdp'}, use_global_device_ids=true, to_apply=%region_2.3 | all-reduce | flops 769 | bytes 6152 | tf_op jit(solution)/shard_map/psum | solution.py:170
  161.2 2.5 collective-permute-start.4
  165.2 47.5 %psum.100 = f32[768]{0:T(1024)S(1)} all-reduce(f32[768]{0:T(1024)S(1)} %fusion.53), channel_id=1, replica_groups=mesh['dp'=4,'fsdp'=8] {'dp','fsdp'}, use_global_device_ids=true, to_apply=%region_6.7 | all-reduce | flops 768 | bytes 6144 | tf_op jit(solution)/shard_map/psum | solution.py:176
  213.3 2.3 collective-permute-start.5
  215.7 2.3 fusion.55
  218.8 20.4 %collective-permute-done.5 = bf16[96,3072]{1,0:T(8,128)(2,1)S(1)} collective-permute-done((bf16[96,3072]{1,0:T(8,128)(2,1)S(1)}, bf16[96,3072]{1,0:T(8,128)(2,1)S(1)}, u32[]{:S(2)}, u32[]{:S(2)}) %collective-permute-start.5) | collective-permute-done | bytes 589856 | tf_op jit(solution)/shard_map/ppermute | solution.py:23
  241.0 29.4 %collective-permute-done.6 = bf16[96,3072]{1,0:T(8,128)(2,1)S(1)} collective-permute-done((bf16[96,3072]{1,0:T(8,128)(2,1)S(1)}, bf16[96,3072]{1,0:T(8,128)(2,1)S(1)}, u32[]{:S(2)}, u32[]{:S(2)}) %collective-permute-start.6) | collective-permute-done | bytes 589856 | tf_op jit(solution)/shard_map/ppermute | solution.py:23
  271.2 9.0 convolution_convert_fusion
  280.2 7.2 copy.50
  287.4 24.2 %while.22 = (s32[]{:T(128)}, bf16[2,512,768]{1,2,0:T(8,128)(2,1)}, f32[2,12,512]{2,1,0:T(8,128)S(1)}, bf16[2,512,2304]{1,2,0:T(8,128)(2,1)}, s32[2,512]{1,0:T(2,128)S(1)}, /*index=5*/s32[]{:T(128)}) while((s32[]{:T(128)}, bf16[2,512,768]{1,2,0:T(8,128)(2,1)}, f32[2,12,512]{2,1,0:T(8,128)S(1)}, bf16[2,512,2304]{1,2,0:T(8,128)(2,1)}, ...), condition=%wide.region_10.11_spmd, body=%wide.region_7.10_spmd.sunk | while | flops 843442688 | bytes 52130384 | solution.py:190
  287.4 2.0 dynamic-slice_bitcast_fusion.6
  289.6 3.1 fusion.131
  292.7 2.6 fusion.132
  295.3 3.3 fusion.133
  299.5 1.8 dynamic-slice_bitcast_fusion.6
  301.5 3.1 fusion.131
  304.6 2.6 fusion.132
  307.2 3.3 fusion.133
  311.7 3.9 fusion.77
  316.1 15.0 %fusion.36 = (u8[512,3072]{1,0:T(8,128)(4,1)S(1)}, u8[512,3072]{1,0:T(8,128)(4,1)S(1)}, f32[2,512,3072]{2,1,0:T(8,128)}) fusion(bf16[768,3072]{1,0:T(8,128)(2,1)} %constant_dynamic-update-slice_fusion.1, f32[2,512,768]{2,1,0:T(8,128)S(1)} %get-tuple-element.175, f32[768]{0:T(1024)S(1)} %copy-done.47, f32[768]{0:T(1024)S(1)} %copy-done.40, ...), kind=kOutput, calls=%fused_computation.80 | convolution fusion | flops 4873519104 | bytes 23607296 | tf_op jit(solution)/shard_map/sjq,qy->sjy/dot_general | solution.py:197
  331.0 31.1 %multiply_convert_fusion.3 = (bf16[2,512,3072]{2,1,0:T(8,128)(2,1)}, f32[2,512,3072]{2,1,0:T(8,128)}) fusion(f32[2,512,3072]{2,1,0:T(8,128)} %get-tuple-element.176, u8[512,3072]{1,0:T(8,128)(4,1)S(1)} %get-tuple-element.99, u8[512,3072]{1,0:T(8,128)(4,1)S(1)} %get-tuple-element.98), kind=kLoop, calls=%fused_computation.37 | loop fusion | flops 220200960 | bytes 34603008 | tf_op jit(solution)/shard_map/convert_element_type | solution.py:203
  362.2 9.5 fusion.78
  372.8 2.4 fusion.34
  375.2 16.4 %add_convert_fusion = bf16[2,512,3072]{2,1,0:T(8,128)(2,1)} fusion(f32[2,512,3072]{2,1,0:T(8,128)} %get-tuple-element.157, f32[2,512,3072]{2,1,0:T(8,128)} %get-tuple-element.176, bf16[3072,768]{1,0:T(8,128)(2,1)} %all-gather.12.cloned.1.call-done, f32[2,512]{1,0:T(2,128)S(1)} %negate_multiply_fusion.2, bf16[2,512,768]{2,1,0:T(8,128)(2,1)} %param.35, ...), kind=kOutput, calls=%fused_computation.36 | convolution fusion | flops 4882956288 | bytes 40913920 | tf_op jit(solution)/shard_map/ivj,hj->ivh/dot_general | solution.py:242
  391.6 11.2 %multiply_reduce_fusion.1 = (bf16[768]{0:T(1024)(128)(2,1)}, f32[2,512]{1,0:T(2,128)S(1)}, bf16[768]{0:T(1024)(128)(2,1)}, f32[2,512,768]{2,1,0:T(8,128)S(1)}) fusion(f32[2,512,768]{2,1,0:T(8,128)} %copy-done.2, f32[2,512]{1,0:T(2,128)S(1)} %fusion.66, f32[2,512]{1,0:T(2,128)S(1)} %broadcast_multiply_fusion.1, f32[768]{0:T(1024)S(1)} %copy-done.40, ...), kind=kOutput, calls=%fused_computation.72 | convolution fusion | flops 4845204480 | bytes 22057984 | tf_op jit(solution)/shard_map/wmx,ix->wmi/dot_general | solution.py:250
  404.1 5.0 bitcast_convert_fusion.3
  409.3 3.9 convolution_convert_fusion.1
  413.2 77.4 %while.23 = (s32[]{:T(128)}, bf16[2,512,2304]{1,2,0:T(8,128)(2,1)}, bf16[2,512,2304]{1,2,0:T(8,128)(2,1)}, s32[2,512]{1,0:T(2,128)S(1)}, f32[2,12,512]{2,1,0:T(8...) while((s32[]{:T(128)}, bf16[2,512,2304]{1,2,0:T(8,128)(2,1)}, bf16[2,512,2304]{1,2,0:T(8,128)(2,1)}, ...), condition=%wide.region_21.22_spmd, body=%wide.region_19.21_spmd.sunk | while | flops 2069490176 | bytes 163754704 | solution.py:267
  413.6 1.8 dynamic-slice_bitcast_fusion.7
  415.6 6.4 fusion.145
  424.4 11.5 %multiply_reduce_fusion.8 = (f32[12,512]{1,0:T(8,128)S(1)}, f32[12,512,512]{1,2,0:T(8,128)}) fusion(f32[12,512,512]{1,2,0:T(8,128)} %fusion.145, f32[12,512]{1,0:T(8,128)S(1)} %dynamic-slice_bitcast_fusion.8, pred[512]{0:T(512)(128)(4,1)S(1)} %compare_reduce_fusion.5, bf16[512,12,64]{0,2,1:T(8,128)(2,1)S(1)} %bitcast.170, ...), kind=kOutput, calls=%fused_computation.14.clone.1 | convolution fusion | flops 418375680 | bytes 26788352 | tf_op jit(solution)/shard_map/while/body/eval_jaxpr/qhe,khe->hqk/dot_general | solution.py:80
  437.1 7.1 multiply_convert_fusion.8
  445.3 2.0 multiply_convert_fusion.9
  447.3 3.1 fusion.146
  451.9 1.8 dynamic-slice_bitcast_fusion.7
  453.9 6.4 fusion.145
  462.7 11.5 %multiply_reduce_fusion.8 = (f32[12,512]{1,0:T(8,128)S(1)}, f32[12,512,512]{1,2,0:T(8,128)}) fusion(f32[12,512,512]{1,2,0:T(8,128)} %fusion.145, f32[12,512]{1,0:T(8,128)S(1)} %dynamic-slice_bitcast_fusion.8, pred[512]{0:T(512)(128)(4,1)S(1)} %compare_reduce_fusion.5, bf16[512,12,64]{0,2,1:T(8,128)(2,1)S(1)} %bitcast.170, ...), kind=kOutput, calls=%fused_computation.14.clone.1 | convolution fusion | flops 418375680 | bytes 26788352 | tf_op jit(solution)/shard_map/while/body/eval_jaxpr/qhe,khe->hqk/dot_general | solution.py:80
  475.5 7.2 multiply_convert_fusion.8
  483.8 2.0 multiply_convert_fusion.9
  485.8 3.1 fusion.146
  490.6 8.5 add_add_fusion.2
  500.8 2.1 fusion.71
  502.9 46.9 %all-reduce.10 = (f32[768]{0:T(1024)}, f32[768]{0:T(1024)}) all-reduce(f32[768]{0:T(1024)} %get-tuple-element.108, f32[768]{0:T(1024)} %get-tuple-element.107), channel_id=1, replica_groups=mesh['dp'=4,'fsdp'=8] {'dp','fsdp'}, use_global_device_ids=true, to_apply=%region_25.26 | all-reduce | flops 1536 | bytes 12288 | tf_op jit(solution)/shard_map/psum | solution.py:281
  555.1 9.0 bitcast_convert_fusion.2
  566.1 11.1 %bitcast_convert_fusion = bf16[3072,768]{1,0:T(8,128)(2,1)} fusion(bf16[2,512,3072]{2,1,0:T(8,128)(2,1)} %get-tuple-element.156, f32[2,512]{1,0:T(2,128)S(1)} %copy-done.50, bf16[2,512,768]{2,1,0:T(8,128)(2,1)} %param.35, f32[2,512,768]{2,1,0:T(8,128)S(1)} %copy-done.1, f32[2,512]{1,0:T(2,128)S(1)} %copy-done.46, f32[768]{0:T(1024)S(1)} %copy-done.27, ...), kind=kOutput, calls=%fused_computation.50 | convolution fusion | flops 4841275392 | bytes 15748096 | tf_op jit(solution)/shard_map/omt,oms->ts/dot_general | solution.py:239
  578.0 10.5 %bitcast_convert_fusion.1 = bf16[768,3072]{1,0:T(8,128)(2,1)} fusion(bf16[2,512,3072]{2,1,0:T(8,128)(2,1)} %add_convert_fusion, f32[2,512,768]{2,1,0:T(8,128)} %copy-done.2, f32[768]{0:T(1024)S(1)} %copy-done.48, f32[768]{0:T(1024)S(1)} %copy-done.41, f32[2,512]{1,0:T(2,128)S(1)} %copy-done.43, f32[2,512]{1,0:T(2,128)S(1)} %copy-done.37), kind=kOutput, calls=%fused_computation.51 | convolution fusion | flops 4838129664 | bytes 14170112 | tf_op jit(solution)/shard_map/oih,oiu->hu/dot_general | solution.py:247
  588.5 2.3 reduce_sum.212
  595.9 37.3 %all-reduce.12 = (bf16[768]{0:T(1024)(128)(2,1)}, bf16[768]{0:T(1024)(128)(2,1)}, bf16[768]{0:T(1024)(128)(2,1)}, bf16[768]{0:T(1024)(128)(2,1)}, bf16[768]{0:T(1024)(128)(2,1)}) all-reduce(bf16[768]{0:T(1024)(128)(2,1)} %dynamic-update-slice.5, bf16[768]{0:T(1024)(128)(2,1)} %get-tuple-element.100, ...), channel_id=1, replica_groups=mesh['dp'=4,'fsdp'=8] {'fsdp'}, use_global_device_ids=true, to_apply=%add.5 | all-reduce | flops 3840 | bytes 15360
  638.3 6.9 all-reduce.14
  651.2 50.9 %reduce-scatter.8.cloned.1.call-done = bf16[96,2304]{1,0:T(8,128)(2,1)} async-done(((bf16[768,2304]{1,0:T(8,128)(2,1)}), bf16[96,2304]{1,0:T(8,128)(2,1)}) %reduce-scatter.8.cloned.1.call-update) | async-done | bytes 442384 | tf_op jit(solution)/shard_map/reduce_scatter | solution.py:321
  702.0 98.5 %reduce-scatter.14.cloned.1.call-done = bf16[384,768]{1,0:T(8,128)(2,1)} async-done(((bf16[3072,768]{1,0:T(8,128)(2,1)}), bf16[384,768]{1,0:T(8,128)(2,1)}) %reduce-scatter.14.cloned.1.call-update) | async-done | bytes 589840 | tf_op jit(solution)/shard_map/reduce_scatter | solution.py:336
  800.6 98.5 %reduce-scatter.12.cloned.1.call-done = bf16[96,3072]{1,0:T(8,128)(2,1)} async-done(((bf16[768,3072]{1,0:T(8,128)(2,1)}), bf16[96,3072]{1,0:T(8,128)(2,1)}) %reduce-scatter.12.cloned.1.call-update) | async-done | bytes 589840 | tf_op jit(solution)/shard_map/reduce_scatter | solution.py:333
  899.1 1.8 convolution_divide_fusion
  900.9 2.2 multiply_add_fusion
  903.8 3.2 convolution_add_fusion
  907.0 44.0 %all-reduce.18.cloned.1.call-done = (bf16[96,768]{1,0:T(8,128)(2,1)}, bf16[96,2304]{1,0:T(8,128)(2,1)}, bf16[96,768]{1,0:T(8,128)(2,1)}, bf16[96,3072]{1,0:T(8,128)(2,1)}, bf16[384,768]{1,0:T(8,128)(2,1)}) async-done(((bf16[96,768]{1,0:T(8,128)(2,1)}, bf16[96,2304]{1,0:T(8,128)(2,1)}, bf16[96,768]{1,0:T(8,128)(2,1)}, bf16[96,3072]{1,0:T(8,128)(2,1)}, bf16[384,768]{1,0:T(8,128)(2,1)}), ...) | async-done | bytes 1916944 | tf_op jit(solution)/shard_map/psum | solution.py:347
  951.0 2.2 convert_element_type.210
  953.2 2.2 convert_element_type.212
  (260 shorter events, 66.1 us)
Async XLA Ops:
  7.2 29.6 %copy-start.53 = (u32[32]{0:T(128)S(1)}, u32[32]{0:T(128)}, u32[]{:S(2)}) copy-start(u32[32]{0:T(128)} %constant.206) | copy-start | bytes 388
  7.2 28.3 %copy-start.60 = (s32[2]{0:T(128)S(1)}, s32[2]{0:T(128)}, u32[]{:S(2)}) copy-start(s32[2]{0:T(128)} %param.32) | copy-start | bytes 28
  7.2 30.9 %copy-start.55 = (bf16[96]{0:T(256)(128)(2,1)S(1)}, bf16[96]{0:T(256)(128)(2,1)}, u32[]{:S(2)}) copy-start(bf16[96]{0:T(256)(128)(2,1)} %param.22) | copy-start | bytes 580
  7.2 31.1 %copy-start.56 = (bf16[96]{0:T(256)(128)(2,1)S(1)}, bf16[96]{0:T(256)(128)(2,1)}, u32[]{:S(2)}) copy-start(bf16[96]{0:T(256)(128)(2,1)} %param.23) | copy-start | bytes 580
  7.2 31.3 %copy-start.57 = (bf16[96]{0:T(256)(128)(2,1)S(1)}, bf16[96]{0:T(256)(128)(2,1)}, u32[]{:S(2)}) copy-start(bf16[96]{0:T(256)(128)(2,1)} %param.26) | copy-start | bytes 580
  7.2 31.6 %copy-start.58 = (bf16[96]{0:T(256)(128)(2,1)S(1)}, bf16[96]{0:T(256)(128)(2,1)}, u32[]{:S(2)}) copy-start(bf16[96]{0:T(256)(128)(2,1)} %param.27) | copy-start | bytes 580
  7.2 31.8 %copy-start.59 = (bf16[96]{0:T(256)(128)(2,1)S(1)}, bf16[96]{0:T(256)(128)(2,1)}, u32[]{:S(2)}) copy-start(bf16[96]{0:T(256)(128)(2,1)} %param.30) | copy-start | bytes 580
  7.3 96.9 %all-gather.6.cloned.1.call-start = ((), (), s32[]{:S(2)}) async-start(), calls=%async_computation.5 | async-start | bytes 1327104 | tf_op jit(solution)/shard_map/all_gather | solution.py:130
  8.0 263.2 %all-gather.8.cloned.1.call-start = ((), (), s32[]{:S(2)}) async-start(), calls=%async_computation.6 | async-start | bytes 3981312 | tf_op jit(solution)/shard_map/all_gather | solution.py:133
  8.7 302.9 %all-gather.10.cloned.1.call-start = ((), (), s32[]{:S(2)}) async-start(), calls=%async_computation.7 | async-start | bytes 1327104 | tf_op jit(solution)/shard_map/all_gather | solution.py:134
  9.5 352.7 %all-gather.12.cloned.1.call-start = ((), (), s32[]{:S(2)}) async-start(), calls=%async_computation.8 | async-start | bytes 5308416 | tf_op jit(solution)/shard_map/all_gather | solution.py:138
  10.0 381.5 %all-gather.14.cloned.1.call-start = ((), (), s32[]{:S(2)}) async-start(), calls=%async_computation.9 | async-start | bytes 5308416 | tf_op jit(solution)/shard_map/all_gather | solution.py:217
  10.1 23.2 %collective-permute-start = (bf16[96,3072]{1,0:T(8,128)(2,1)}, bf16[96,3072]{1,0:T(8,128)(2,1)S(1)}, u32[]{:S(2)}, u32[]{:S(2)}) collective-permute-start(bf16[96,3072]{1,0:T(8,128)(2,1)} %param.28), channel_id=1, source_target_pairs={{0,1},{1,2},{2,3},{3,4},{4,5},{5,6},{6,7},{7,0},{8,9},{9,10},{10,1... | collective-permute-start | bytes 1769480 | tf_op jit(solution)/shard_map/ppermute | solution.py:23
  13.1 638.0 %reduce-scatter.10.cloned.1.call-start = ((), (), s32[]{:S(2)}) async-start(), calls=%async_computation.12 | async-start | bytes 1327104 | tf_op jit(solution)/shard_map/reduce_scatter | solution.py:324
  14.1 24.0 %copy-start.54 = (f32[2,128]{1,0:T(2,128)}, f32[2,128]{1,0:T(2,128)S(1)}, u32[]{:S(2)}) copy-start(f32[2,128]{1,0:T(2,128)S(1)} %broadcast_maximum_fusion) | copy-start | bytes 3076
  33.3 53.4 %collective-permute-start.1 = (bf16[96,3072]{1,0:T(8,128)(2,1)S(1)}, bf16[96,3072]{1,0:T(8,128)(2,1)S(1)}, u32[]{:S(2)}, u32[]{:S(2)}) collective-permute-start(bf16[96,3072]{1,0:T(8,128)(2,1)S(1)} %collective-permute-done), channel_id=1, source_target_pairs={{0,1},{1,2},{2,3},{3,4},{4,5},{5,6},{6,7},{7,0},{8,9},{9,10},{10,1... | collective-permute-start | bytes 1769480 | tf_op jit(solution)/shard_map/ppermute | solution.py:23
  35.3 68.8 %copy-start.15 = (bf16[2,128,768]{2,1,0:T(8,128)(2,1)}, bf16[2,128,768]{2,1,0:T(8,128)(2,1)S(1)}, u32[]{:S(2)}) copy-start(bf16[2,128,768]{2,1,0:T(8,128)(2,1)S(1)} %fusion.47) | copy-start | bytes 1179652
  35.3 50.4 %copy-start.12 = (bf16[96,3072]{1,0:T(8,128)(2,1)S(1)}, bf16[96,3072]{1,0:T(8,128)(2,1)}, u32[]{:S(2)}) copy-start(bf16[96,3072]{1,0:T(8,128)(2,1)} %param.28) | copy-start | bytes 1769476
  80.7 135.0 %copy-start.34 = (f32[768]{0:T(1024)}, f32[768]{0:T(1024)S(1)}, u32[]{:S(2)}) copy-start(f32[768]{0:T(1024)S(1)} %convert_element_type.182) | copy-start | bytes 9220
  86.6 129.0 %copy-start.30 = (s32[2,512]{1,0:T(2,128)S(1)}, s32[2,512]{1,0:T(2,128)}, u32[]{:S(2)}) copy-start(s32[2,512]{1,0:T(2,128)} %param.33) | copy-start | bytes 12292
  86.6 16.6 %collective-permute-start.2 = (bf16[96,3072]{1,0:T(8,128)(2,1)S(1)}, bf16[96,3072]{1,0:T(8,128)(2,1)S(1)}, u32[]{:S(2)}, u32[]{:S(2)}) collective-permute-start(bf16[96,3072]{1,0:T(8,128)(2,1)S(1)} %collective-permute-done.1), channel_id=1, source_target_pairs={{0,1},{1,2},{2,3},{3,4},{4,5},{5,6},{6,7},{7,0},{8,9},{9,10},{10,1... | collective-permute-start | bytes 1769480 | tf_op jit(solution)/shard_map/ppermute | solution.py:23
  103.2 58.0 %collective-permute-start.3 = (bf16[96,3072]{1,0:T(8,128)(2,1)S(1)}, bf16[96,3072]{1,0:T(8,128)(2,1)S(1)}, u32[]{:S(2)}, u32[]{:S(2)}) collective-permute-start(bf16[96,3072]{1,0:T(8,128)(2,1)S(1)} %collective-permute-done.2), channel_id=1, source_target_pairs={{0,1},{1,2},{2,3},{3,4},{4,5},{5,6},{6,7},{7,0},{8,9},{9,10},{10,1... | collective-permute-start | bytes 1769480 | tf_op jit(solution)/shard_map/ppermute | solution.py:23
  105.9 134.3 %copy-start.4 = (f32[2,128,768]{2,1,0:T(8,128)}, f32[2,128,768]{2,1,0:T(8,128)S(1)}, u32[]{:S(2)}) copy-start(f32[2,128,768]{2,1,0:T(8,128)S(1)} %get-tuple-element.173) | copy-start | bytes 2359300
  161.2 52.1 %collective-permute-start.4 = (bf16[96,3072]{1,0:T(8,128)(2,1)S(1)}, bf16[96,3072]{1,0:T(8,128)(2,1)S(1)}, u32[]{:S(2)}, u32[]{:S(2)}) collective-permute-start(bf16[96,3072]{1,0:T(8,128)(2,1)S(1)} %collective-permute-done.3), channel_id=1, source_target_pairs={{0,1},{1,2},{2,3},{3,4},{4,5},{5,6},{6,7},{7,0},{8,9},{9,10},{10,1... | collective-permute-start | bytes 1769480 | tf_op jit(solution)/shard_map/ppermute | solution.py:23
  164.4 75.8 %copy-start.24 = (f32[768]{0:T(1024)}, f32[768]{0:T(1024)S(1)}, u32[]{:S(2)}) copy-start(f32[768]{0:T(1024)S(1)} %broadcast_divide_fusion.1) | copy-start | bytes 9220
  213.3 27.7 %copy-start.32 = (f32[768]{0:T(1024)}, f32[768]{0:T(1024)S(1)}, u32[]{:S(2)}) copy-start(f32[768]{0:T(1024)S(1)} %add_rsqrt_fusion) | copy-start | bytes 9220
  213.3 57.9 %copy-start.13 = (bf16[2,512,768]{2,1,0:T(8,128)(2,1)S(1)}, bf16[2,512,768]{2,1,0:T(8,128)(2,1)}, u32[]{:S(2)}) copy-start(bf16[2,512,768]{2,1,0:T(8,128)(2,1)} %param.20) | copy-start | bytes 4718596
  213.3 25.9 %collective-permute-start.5 = (bf16[96,3072]{1,0:T(8,128)(2,1)S(1)}, bf16[96,3072]{1,0:T(8,128)(2,1)S(1)}, u32[]{:S(2)}, u32[]{:S(2)}) collective-permute-start(bf16[96,3072]{1,0:T(8,128)(2,1)S(1)} %collective-permute-done.4), channel_id=1, source_target_pairs={{0,1},{1,2},{2,3},{3,4},{4,5},{5,6},{6,7},{7,0},{8,9},{9,10},{10,1... | collective-permute-start | bytes 1769480 | tf_op jit(solution)/shard_map/ppermute | solution.py:23
  239.2 31.1 %collective-permute-start.6 = (bf16[96,3072]{1,0:T(8,128)(2,1)S(1)}, bf16[96,3072]{1,0:T(8,128)(2,1)S(1)}, u32[]{:S(2)}, u32[]{:S(2)}) collective-permute-start(bf16[96,3072]{1,0:T(8,128)(2,1)S(1)} %collective-permute-done.5), channel_id=1, source_target_pairs={{0,1},{1,2},{2,3},{3,4},{4,5},{5,6},{6,7},{7,0},{8,9},{9,10},{10,1... | collective-permute-start | bytes 1769480 | tf_op jit(solution)/shard_map/ppermute | solution.py:23
  280.2 7.2 copy-start.20
  280.2 7.2 copy-start.23
  287.4 24.3 %copy-start.7 = (f32[2,512,768]{2,1,0:T(8,128)S(1)}, f32[2,512,768]{2,1,0:T(8,128)}, u32[]{:S(2)}) copy-start(f32[2,512,768]{2,1,0:T(8,128)} %fusion.55) | copy-start | bytes 9437188
  315.5 15.5 %copy-start.2 = (f32[2,512,768]{2,1,0:T(8,128)}, f32[2,512,768]{2,1,0:T(8,128)S(1)}, u32[]{:S(2)}) copy-start(f32[2,512,768]{2,1,0:T(8,128)S(1)} %get-tuple-element.175) | copy-start | bytes 9437188
  315.6 87.3 %copy-start.36 = (f32[2,512]{1,0:T(2,128)}, f32[2,512]{1,0:T(2,128)S(1)}, u32[]{:S(2)}) copy-start(f32[2,512]{1,0:T(2,128)S(1)} %broadcast_multiply_fusion.1) | copy-start | bytes 12292
  316.1 86.8 %copy-start.42 = (f32[2,512]{1,0:T(2,128)}, f32[2,512]{1,0:T(2,128)S(1)}, u32[]{:S(2)}) copy-start(f32[2,512]{1,0:T(2,128)S(1)} %fusion.66) | copy-start | bytes 12292
  362.1 9.6 copy-start.6
  362.1 9.6 copy-start.26
  371.7 19.9 %copy-start = (f32[2,512,768]{2,1,0:T(8,128)}, f32[2,512,768]{2,1,0:T(8,128)S(1)}, u32[]{:S(2)}) copy-start(f32[2,512,768]{2,1,0:T(8,128)S(1)} %get-tuple-element.178) | copy-start | bytes 9437188
  371.7 19.8 %copy-start.28 = (f32[2,512]{1,0:T(2,128)}, f32[2,512]{1,0:T(2,128)S(1)}, u32[]{:S(2)}) copy-start(f32[2,512]{1,0:T(2,128)S(1)} %broadcast_multiply_fusion) | copy-start | bytes 12292
  372.8 18.8 %copy-start.38 = (f32[2,512]{1,0:T(2,128)}, f32[2,512]{1,0:T(2,128)S(1)}, u32[]{:S(2)}) copy-start(f32[2,512]{1,0:T(2,128)S(1)} %get-tuple-element.169) | copy-start | bytes 12292
  372.8 18.8 %copy-start.45 = (f32[2,512]{1,0:T(2,128)}, f32[2,512]{1,0:T(2,128)S(1)}, u32[]{:S(2)}) copy-start(f32[2,512]{1,0:T(2,128)S(1)} %get-tuple-element.168) | copy-start | bytes 12292
  375.2 16.4 %copy-start.49 = (f32[2,512]{1,0:T(2,128)}, f32[2,512]{1,0:T(2,128)S(1)}, u32[]{:S(2)}) copy-start(f32[2,512]{1,0:T(2,128)S(1)} %negate_multiply_fusion.2) | copy-start | bytes 12292
  391.6 11.3 %copy-start.3 = (f32[2,512,768]{2,1,0:T(8,128)S(1)}, f32[2,512,768]{2,1,0:T(8,128)}, u32[]{:S(2)}) copy-start(f32[2,512,768]{2,1,0:T(8,128)} %copy-done.2) | copy-start | bytes 9437188
  409.2 242.0 %reduce-scatter.6.cloned.1.call-start = ((), (), s32[]{:S(2)}) async-start(), calls=%async_computation.10 | async-start | bytes 1327104 | tf_op jit(solution)/shard_map/reduce_scatter | solution.py:318
  413.2 77.4 %copy-start.52 = (f32[2,512]{1,0:T(2,128)S(1)}, f32[2,512]{1,0:T(2,128)}, u32[]{:S(2)}) copy-start(f32[2,512]{1,0:T(2,128)} %copy-done.51) | copy-start | bytes 12292
  424.4 11.5 %slice-start = ((s8[12582912]{0:T(1024)(128)(4,1)}), s8[4194304]{0:T(1024)(128)(4,1)S(1)}, s32[]{:S(2)}) async-start(s8[12582912]{0:T(1024)(128)(4,1)} %bitcast.162), calls=%async_computation.16 | async-start | bytes 8388608 | tf_op jit(solution)/shard_map/while
  424.4 11.5 %slice-start.1 = ((s8[12582912]{0:T(1024)(128)(4,1)}), s8[4194304]{0:T(1024)(128)(4,1)S(1)}, s32[]{:S(2)}) async-start(s8[12582912]{0:T(1024)(128)(4,1)} %bitcast.162), calls=%async_computation.17 | async-start | bytes 8388608 | tf_op jit(solution)/shard_map/while
  424.4 12.7 %slice-start.2 = ((s8[12582912]{0:T(1024)(128)(4,1)}), s8[4194304]{0:T(1024)(128)(4,1)S(1)}, s32[]{:S(2)}) async-start(s8[12582912]{0:T(1024)(128)(4,1)} %bitcast.162), calls=%async_computation.18 | async-start | bytes 8388608 | tf_op jit(solution)/shard_map/while
  453.9 6.4 copy-start.10
  462.7 11.5 %slice-start = ((s8[12582912]{0:T(1024)(128)(4,1)}), s8[4194304]{0:T(1024)(128)(4,1)S(1)}, s32[]{:S(2)}) async-start(s8[12582912]{0:T(1024)(128)(4,1)} %bitcast.162), calls=%async_computation.16 | async-start | bytes 8388608 | tf_op jit(solution)/shard_map/while
  462.7 11.5 %slice-start.1 = ((s8[12582912]{0:T(1024)(128)(4,1)}), s8[4194304]{0:T(1024)(128)(4,1)S(1)}, s32[]{:S(2)}) async-start(s8[12582912]{0:T(1024)(128)(4,1)} %bitcast.162), calls=%async_computation.17 | async-start | bytes 8388608 | tf_op jit(solution)/shard_map/while
  462.7 12.7 %slice-start.2 = ((s8[12582912]{0:T(1024)(128)(4,1)}), s8[4194304]{0:T(1024)(128)(4,1)S(1)}, s32[]{:S(2)}) async-start(s8[12582912]{0:T(1024)(128)(4,1)} %bitcast.162), calls=%async_computation.18 | async-start | bytes 8388608 | tf_op jit(solution)/shard_map/while
  490.6 10.2 %copy-start.5 = (f32[2,128,768]{2,1,0:T(8,128)S(1)}, f32[2,128,768]{2,1,0:T(8,128)}, u32[]{:S(2)}) copy-start(f32[2,128,768]{2,1,0:T(8,128)} %copy-done.4) | copy-start | bytes 2359300
  490.6 10.2 %copy-start.25 = (f32[768]{0:T(1024)S(1)}, f32[768]{0:T(1024)}, u32[]{:S(2)}) copy-start(f32[768]{0:T(1024)} %copy-done.24) | copy-start | bytes 9220
  490.6 10.2 %copy-start.31 = (s32[2,512]{1,0:T(2,128)S(1)}, s32[2,512]{1,0:T(2,128)}, u32[]{:S(2)}) copy-start(s32[2,512]{1,0:T(2,128)} %param.33) | copy-start | bytes 12292
  490.6 10.2 %copy-start.33 = (f32[768]{0:T(1024)S(1)}, f32[768]{0:T(1024)}, u32[]{:S(2)}) copy-start(f32[768]{0:T(1024)} %copy-done.32) | copy-start | bytes 9220
  500.8 50.4 %copy-start.35 = (f32[768]{0:T(1024)S(1)}, f32[768]{0:T(1024)}, u32[]{:S(2)}) copy-start(f32[768]{0:T(1024)} %copy-done.34) | copy-start | bytes 9220
  500.8 52.7 %copy-start.16 = (bf16[2,128,768]{2,1,0:T(8,128)(2,1)S(1)}, bf16[2,128,768]{2,1,0:T(8,128)(2,1)}, u32[]{:S(2)}) copy-start(bf16[2,128,768]{2,1,0:T(8,128)(2,1)} %copy-done.15) | copy-start | bytes 1179652
  502.9 52.2 %copy-start.14 = (bf16[2,512,768]{2,1,0:T(8,128)(2,1)S(1)}, bf16[2,512,768]{2,1,0:T(8,128)(2,1)}, u32[]{:S(2)}) copy-start(bf16[2,512,768]{2,1,0:T(8,128)(2,1)} %param.20) | copy-start | bytes 4718596
  555.1 147.0 %reduce-scatter.8.cloned.1.call-start = ((), (), s32[]{:S(2)}) async-start(), calls=%async_computation.11 | async-start | bytes 3981312 | tf_op jit(solution)/shard_map/reduce_scatter | solution.py:321
  564.2 236.3 %reduce-scatter.14.cloned.1.call-start = ((), (), s32[]{:S(2)}) async-start(), calls=%async_computation.14 | async-start | bytes 5308416 | tf_op jit(solution)/shard_map/reduce_scatter | solution.py:336
  577.3 321.8 %reduce-scatter.12.cloned.1.call-start = ((), (), s32[]{:S(2)}) async-start(), calls=%async_computation.13 | async-start | bytes 5308416 | tf_op jit(solution)/shard_map/reduce_scatter | solution.py:333
  588.4 310.7 %copy-start.18 = (bf16[2,128,768]{2,1,0:T(8,128)(2,1)S(1)}, bf16[2,128,768]{2,1,0:T(8,128)(2,1)}, u32[]{:S(2)}) copy-start(bf16[2,128,768]{2,1,0:T(8,128)(2,1)} %copy-done.17) | copy-start | bytes 1179652
  588.4 362.5 %all-reduce.18.cloned.1.call-start = ((), (), s32[]{:S(2)}) async-start(), calls=%async_computation.15 | async-start | bytes 3833856 | tf_op jit(solution)/shard_map/psum | solution.py:347
  (22 other events, 62.6 us)
Sparse Core Ops, SparseCore 0:
  10.3 51.0 all-gather.5
  63.6 82.8 all-gather.7
  148.7 44.5 all-gather.9
  195.3 99.0 all-gather.11
  296.4 77.9 all-gather.13
  409.3 71.1 reduce-scatter.9
  555.2 64.8 reduce-scatter.5
  623.7 78.2 reduce-scatter.7
  705.7 94.8 reduce-scatter.13
  804.0 94.9 reduce-scatter.11
  901.8 49.1 all-reduce.17
